TPU v7x, 32 devices: a whole 2x2x4 slice. The times are simulated.
32 devices in a mesh: expert: 16 (over z, y, x), dp: 2 (over core).
Axes of the slice: x: 2, y: 2, z: 4, core: 2. Of those that a mesh axis runs over, the one named last changes fastest.
Arguments:
- tokens: bfloat16 [1024, 3584], P(('dp', 'expert')), parts along dimension 0, may hold values from -6 to 6
- expert_ids: int32 [1024, 8], P(('dp', 'expert')), parts along dimension 0, may hold values from 0 to 11, as said below
- gate_weights: float32 [1024, 8], P(('dp', 'expert')), parts along dimension 0, may hold values from 0.05 to 0.5
- placement_table: int32 [24, 2], P('dp'), parts along dimension 0, may hold values from 0 to 15, as said below
- replica_choice: int32 [1024, 8], P(('dp', 'expert')), parts along dimension 0, may hold values from 0 to 1
- w_gate: bfloat16 [16, 3584, 1024], P('expert'), may hold values from -0.09375 to 0.09375
- w_up: bfloat16 [16, 3584, 1024], P('expert'), may hold values from -0.09375 to 0.09375
- w_down: bfloat16 [16, 1024, 3584], P('expert'), may hold values from -0.1875 to 0.1875
Outputs:
- mixed: bfloat16 [1024, 3584], P(('dp', 'expert')), parts along dimension 0
- slot_load: float32 [32], P(('dp', 'expert')), parts along dimension 0
There are 2 independent parts, one for each index of `dp`. A program takes and returns all parts, laid end to end along the dimension named above; an argument that names none is the same for every part. Nothing has to cross between parts.
Inputs may be any that keep to these rules, and one draw needn't show every extreme that they name: `expert_ids`: each row names 8 different logical experts, hot experts chosen more often. `placement_table`: every slot of 0 to 15 appears for exactly one expert; 4 experts have two different slots, every other expert has the same slot in both columns. `replica_choice`: a column of the placement table.
All inputs are finite; a program needn't handle non-finite values.
Results may differ from a plain program's by a relative error of at most 0.0025.
Values may be sent and summed in bfloat16 or wider, within the bound.
A program may use at most 128 MiB of HBM per device.

v0:
```python
import jax
import jax.numpy as jnp
from jax import lax
from jax.sharding import PartitionSpec as P


def run_experts(received, gate_w, up_w, down_w):
    peers, capacity, hidden_dimension = received.shape
    rows = received.reshape(peers * capacity, hidden_dimension)
    gate_part = jnp.dot(rows, gate_w, preferred_element_type=jnp.float32)
    up_part = jnp.dot(rows, up_w, preferred_element_type=jnp.float32)
    hidden = (jax.nn.silu(gate_part) * up_part).astype(jnp.bfloat16)
    output = jnp.dot(hidden, down_w, preferred_element_type=jnp.float32).astype(jnp.bfloat16)
    return output.reshape(peers, capacity, hidden_dimension)


def per_device(
    tokens, expert_ids, gate_weights, placement_table, replica_choice, w_gate, w_up, w_down
):
    devices = lax.axis_size("expert")
    tok_rows, top_count = expert_ids.shape
    hidden_dimension = tokens.shape[1]
    slot_total = devices
    capacity = 5 * tok_rows * top_count // (4 * slot_total) + 1
    slot_ids = placement_table[expert_ids, replica_choice].astype(jnp.int32).reshape(-1)
    onehot = (slot_ids[:, None] == jnp.arange(slot_total, dtype=jnp.int32)[None, :]).astype(
        jnp.int32
    )
    running = jnp.cumsum(onehot, axis=0)
    position = jnp.sum(running * onehot, axis=1) - 1
    retained_selector = position < capacity
    table_rows = slot_total * capacity
    flat = jnp.where(retained_selector, slot_ids * capacity + position, table_rows)
    token_index = jnp.arange(tok_rows * top_count, dtype=jnp.int32) // top_count
    source_item_index = (
        jnp.full((table_rows,), tok_rows, jnp.int32).at[flat].set(token_index, mode="drop")
    )
    padded = jnp.concatenate([tokens, jnp.zeros((1, hidden_dimension), tokens.dtype)], axis=0)
    outgoing = padded[source_item_index].reshape(devices, capacity, hidden_dimension)
    gate_w = w_gate[0]
    up_w = w_up[0]
    down_w = w_down[0]
    incoming = lax.all_to_all(outgoing, "expert", split_axis=0, concat_axis=0, tiled=True)
    results = run_experts(incoming, gate_w, up_w, down_w)
    returned = lax.all_to_all(results, "expert", split_axis=0, concat_axis=0, tiled=True)
    returned = returned.reshape(table_rows, hidden_dimension)
    pair_rows = returned[jnp.minimum(flat, table_rows - 1)].reshape(
        tok_rows, top_count, hidden_dimension
    )
    weights = jnp.where(retained_selector.reshape(tok_rows, top_count), gate_weights, 0.0).astype(
        jnp.float32
    )
    mixed = jnp.sum(weights[:, :, None] * pair_rows.astype(jnp.float32), axis=1).astype(
        jnp.bfloat16
    )
    counts = jnp.sum(onehot * retained_selector.astype(jnp.int32)[:, None], axis=0).astype(
        jnp.float32
    )
    own_counts = lax.psum_scatter(counts, "expert", scatter_dimension=0, tiled=True)
    slot_load = own_counts * (slot_total / (tok_rows * devices * top_count))
    return (mixed, slot_load)


def solution(mesh):
    placed = (
        P(("dp", "expert"), None),
        P(("dp", "expert"), None),
        P(("dp", "expert"), None),
        P("dp", None),
        P(("dp", "expert"), None),
        P("expert", None, None),
        P("expert", None, None),
        P("expert", None, None),
    )
    return jax.shard_map(
        per_device,
        mesh=mesh,
        in_specs=placed,
        out_specs=(P(("dp", "expert"), None), P(("dp", "expert"))),
        check_vma=False,
    )
```

profile of v0, /device:TPU:6, one launch (start us, length us, event | category | flops | bytes accessed | tf_op | source)
XLA Modules:
  0.0 209.8 jit_solution(3355897944623513293)
XLA Ops:
  0.6 0.0 copy-start
  0.7 0.7 fusion.23
  1.4 0.1 copy.14
  1.4 0.1 reshape.112
  1.5 0.0 copy-done
  1.5 0.0 copy-start.1
  1.6 2.4 %gather_fusion = s32[256]{0:T(256)S(1)} fusion(s32[12,2]{0,1:T(2,128)S(1)} %copy-done, s32[256]{0:T(256)S(1)} %reshape.112), kind=kCustom, calls=%fused_computation | custom fusion | bytes 4096 | tf_op jit(solution)/shard_map/gather | solution.py:25
  4.0 0.6 reduce-window.6
  4.6 0.2 slice_reduce_fusion
  4.8 0.1 fusion.19
  4.9 1.4 scatter_custom_fusion
  6.3 0.0 copy-done.1
  6.4 3.8 %gather_fusion.1 = bf16[336,3584]{1,0:T(8,128)(2,1)} fusion(bf16[33,3584]{1,0:T(8,128)(2,1)S(1)} %concatenate.7, s32[1024]{0:T(1024)S(1)} %pad_clamp_fusion.1), kind=kCustom, calls=%fused_computation.1 | custom fusion | bytes 4818240 | tf_op jit(solution)/shard_map/gather | solution.py:39
  10.2 2.1 reshape.107
  12.2 68.8 %all_to_all.10 = bf16[16,21,3584]{2,1,0:T(8,128)(2,1)} all-to-all(bf16[16,21,3584]{2,1,0:T(8,128)(2,1)S(1)} %reshape.107), channel_id=1, replica_groups=mesh['expert'=16,'dp'=2] {'expert'}, dimensions={0} | all-to-all | bytes 4816896 | tf_op jit(solution)/shard_map/all_to_all | solution.py:43
  81.1 2.2 %reshape.108 = bf16[336,3584]{1,0:T(8,128)(2,1)S(1)} reshape(bf16[16,21,3584]{2,1,0:T(8,128)(2,1)} %all_to_all.10) | data formatting | bytes 4816896 | tf_op jit(solution)/shard_map/reshape | solution.py:9
  83.2 7.0 %fusion.4 = f32[336,1024]{1,0:T(8,128)} fusion(bf16[336,3584]{1,0:T(8,128)(2,1)S(1)} %reshape.108, bf16[1,3584,1024]{2,1,0:T(8,128)(2,1)} %param.13), kind=kOutput, calls=%fused_computation.8 | convolution fusion | flops 2466250752 | bytes 11124736 | tf_op jit(solution)/shard_map/dot_general | solution.py:10
  90.2 12.4 %fusion.6 = bf16[336,3584]{1,0:T(8,128)(2,1)} fusion(bf16[1,1024,3584]{2,1,0:T(8,128)(2,1)} %param.15, bf16[336,3584]{1,0:T(8,128)(2,1)S(1)} %reshape.108, bf16[1,3584,1024]{2,1,0:T(8,128)(2,1)} %param.14, f32[336,1024]{1,0:T(8,128)} %fusion.4), kind=kOutput, calls=%fused_computation.10 | convolution fusion | flops 4935770112 | bytes 20873216 | tf_op jit(solution)/shard_map/dot_general | solution.py:13
  102.6 3.2 %reshape.109 = bf16[16,21,3584]{2,1,0:T(8,128)(2,1)} reshape(bf16[336,3584]{1,0:T(8,128)(2,1)} %fusion.6) | data formatting | bytes 4816896 | tf_op jit(solution)/shard_map/reshape | solution.py:14
  105.8 0.0 copy-start.2
  105.8 0.0 copy-start.3
  105.8 8.7 %all-to-all-start.1 = ((bf16[16,21,3584]{2,1,0:T(8,128)(2,1)}), bf16[16,21,3584]{2,1,0:T(8,128)(2,1)}, u32[]{:S(2)}, u32[]{:S(2)}) async-start(bf16[16,21,3584]{2,1,0:T(8,128)(2,1)} %reshape.109), calls=%async_computation.1 | async-start | bytes 5505024 | tf_op jit(solution)/shard_map/all_to_all | solution.py:45
  114.5 0.1 lt.58
  114.6 0.0 copy-done.2
  114.6 0.1 copy.16
  114.7 0.1 select_reduce_fusion
  114.8 0.0 copy-done.3
  114.8 0.6 dynamic-slice
  115.4 82.5 %all-reduce.1 = f32[16]{0:T(128)S(1)} all-reduce(f32[16]{0:T(128)S(1)} %convert_element_type.37), channel_id=2, replica_groups=mesh['expert'=16,'dp'=2] {'expert'}, use_global_device_ids=true, to_apply=%region_6.7.clone | all-reduce | flops 16 | bytes 128
  197.9 1.2 dynamic-slice.1
  199.8 0.0 all-to-all-done.1
  199.8 2.2 %reshape.110 = bf16[336,3584]{1,0:T(8,128)(2,1)S(1)} reshape(bf16[16,21,3584]{2,1,0:T(8,128)(2,1)} %all-to-all-done.1) | data formatting | bytes 4816896 | tf_op jit(solution)/shard_map/reshape | solution.py:46
  202.0 3.0 %gather_fusion.2 = bf16[256,3584]{1,0:T(8,128)(2,1)} fusion(bf16[336,3584]{1,0:T(8,128)(2,1)S(1)} %reshape.110, s32[1024]{0:T(1024)S(1)} %pad_clamp_fusion), kind=kCustom, calls=%fused_computation.2 | custom fusion | bytes 3671040 | tf_op jit(solution)/shard_map/gather | solution.py:47
  205.0 3.6 %fusion.9 = bf16[32,3584]{1,0:T(8,128)(2,1)} fusion(bf16[256,3584]{1,0:T(8,128)(2,1)} %gather_fusion.2, f32[32,8]{1,0:T(8,128)S(1)} %broadcast_select_fusion), kind=kLoop, calls=%fused_computation.12 | loop fusion | flops 2637824 | bytes 2065408 | tf_op jit(solution)/shard_map/reduce_sum | solution.py:53
  (13 shorter events, 0.1 us)
Async XLA Ops:
  0.6 0.9 copy-start
  1.5 4.8 %copy-start.1 = (bf16[32,3584]{1,0:T(8,128)(2,1)S(1)}, bf16[32,3584]{1,0:T(8,128)(2,1)}, u32[]{:S(2)}) copy-start(bf16[32,3584]{1,0:T(8,128)(2,1)} %param.8) | copy-start | bytes 688132
  105.8 8.8 %copy-start.2 = (f32[32,8]{0,1:T(8,128)S(1)}, f32[32,8]{0,1:T(8,128)}, u32[]{:S(2)}) copy-start(f32[32,8]{0,1:T(8,128)} %param.10) | copy-start | bytes 3076
  105.8 9.0 %copy-start.3 = (u32[32]{0:T(128)S(1)}, u32[32]{0:T(128)}, u32[]{:S(2)}) copy-start(u32[32]{0:T(128)} %constant.73) | copy-start | bytes 388
  105.8 94.0 %all-to-all-start.1 = ((bf16[16,21,3584]{2,1,0:T(8,128)(2,1)}), bf16[16,21,3584]{2,1,0:T(8,128)(2,1)}, u32[]{:S(2)}, u32[]{:S(2)}) async-start(bf16[16,21,3584]{2,1,0:T(8,128)(2,1)} %reshape.109), calls=%async_computation.1 | async-start | bytes 5505024 | tf_op jit(solution)/shard_map/all_to_all | solution.py:45
where the time goes:
time: 213 us; the launch traced here: 210 us
  blocking collectives  151 us (71%)
  local copies, waits for them, and re-layouts  22.6 us (11%)
  matrix products  19.4 us (9%)
  starting transfers between devices  8.67 us (4%)
  other arithmetic  5.25 us (2%)
  between operations  2.59 us (1%)
    unnamed x1, blocking collectives  82.5 us
    all_to_all x1, blocking collectives, per_device(): lax.all_to_all(outgoing, 'expert', split_axis=0, concat_axis=0, tiled=True)  68.8 us
    dot_general x1, matrix products, run_experts(): jnp.dot(hidden, down_w, preferred_element_type=jnp.float32)  12.4 us
    all_to_all x1, starting transfers between devices, per_device(): lax.all_to_all(results, 'expert', split_axis=0, concat_axis=0, tiled=True)  8.67 us
    dot_general x1, matrix products, run_experts(): gate_part = jnp.dot(rows, gate_w, preferred_element_type=jnp.float32)  6.95 us
  transfers between devices with their start and end apart: 1, of which 0 were waited for; matrix products, arithmetic and copies ran while one was open for 1% of the time, Pallas kernels for 0%

commit v1 on v0

--- a/solution.py
+++ b/solution.py
@@ -1,7 +1,15 @@
+import functools
+
 import jax
 import jax.numpy as jnp
 from jax import lax
+from jax.experimental import pallas as pl
+from jax.experimental.pallas import tpu as pltpu
 from jax.sharding import PartitionSpec as P
+
+PLANE = 4
+LANES = 128
+VMEM_BYTES = 64 * 1000 * 1000
 
 
 def run_experts(received, gate_w, up_w, down_w):
@@ -14,7 +22,7 @@
     return output.reshape(peers, capacity, hidden_dimension)
 
 
-def per_device(
+def per_device_exchange(
     tokens, expert_ids, gate_weights, placement_table, replica_choice, w_gate, w_up, w_down
 ):
     devices = lax.axis_size("expert")
@@ -37,11 +45,8 @@
     )
     padded = jnp.concatenate([tokens, jnp.zeros((1, hidden_dimension), tokens.dtype)], axis=0)
     outgoing = padded[source_item_index].reshape(devices, capacity, hidden_dimension)
-    gate_w = w_gate[0]
-    up_w = w_up[0]
-    down_w = w_down[0]
     incoming = lax.all_to_all(outgoing, "expert", split_axis=0, concat_axis=0, tiled=True)
-    results = run_experts(incoming, gate_w, up_w, down_w)
+    results = run_experts(incoming, w_gate[0], w_up[0], w_down[0])
     returned = lax.all_to_all(results, "expert", split_axis=0, concat_axis=0, tiled=True)
     returned = returned.reshape(table_rows, hidden_dimension)
     pair_rows = returned[jnp.minimum(flat, table_rows - 1)].reshape(
@@ -59,6 +64,338 @@
     own_counts = lax.psum_scatter(counts, "expert", scatter_dimension=0, tiled=True)
     slot_load = own_counts * (slot_total / (tok_rows * devices * top_count))
     return (mixed, slot_load)
+
+
+def tile_of(size, wanted):
+    tile = min(size, wanted)
+    while size % tile:
+        tile -= LANES
+    return tile
+
+
+def kernel(
+    n, rows, top, cap, depth, hidden,
+    ext_ref, gates_ref, wg_hbm, wu_hbm, wd_hbm,
+    mixed_ref, load_ref,
+    gathered, wg, wu, wd, packed, mid, outgoing, incoming, acc,
+    w_sem, own_sem, ag_send, ag_recv, ret_send, ret_recv, local_sem,
+):
+    planes = n // PLANE
+    pad = outgoing.shape[1] * outgoing.shape[2]
+    me = lax.axis_index("expert")
+    z = me // PLANE
+    q = me % PLANE
+    y, x = q // 2, q % 2
+    x_peer = y * 2 + (1 - x)
+    y_peer = (1 - y) * 2 + x
+    d_peer = (1 - y) * 2 + (1 - x)
+    half = rows // 2
+
+    weight_copies = [
+        pltpu.make_async_copy(src.at[0], dst, w_sem.at[i])
+        for i, (src, dst) in enumerate(((wg_hbm, wg), (wu_hbm, wu), (wd_hbm, wd)))
+    ]
+    own = pltpu.make_async_copy(ext_ref, gathered.at[me], own_sem)
+    own.start()
+    for copy in weight_copies:
+        copy.start()
+
+    barrier = pltpu.get_barrier_semaphore()
+    for other in range(1, n):
+        pl.semaphore_signal(
+            barrier, inc=1, device_id={"expert": lax.rem(me + other, n)},
+            device_id_type=pl.DeviceIdType.MESH,
+        )
+    pl.semaphore_wait(barrier, n - 1)
+    own.wait()
+
+    def send(group, plane, kind_send, kind_recv, target, first=0, count=None):
+        count = rows if count is None else count
+        part = gathered.at[group, pl.ds(first, count)]
+        return pltpu.make_async_remote_copy(
+            src_ref=part, dst_ref=part,
+            send_sem=ag_send.at[plane, kind_send], recv_sem=ag_recv.at[plane, kind_recv],
+            device_id={"expert": target}, device_id_type=pl.DeviceIdType.MESH,
+        )
+
+    def plane_at(b):
+        low = jnp.minimum(z, planes - 1 - z)
+        near = low + ((b + 1) // 2) * (1 if b % 2 else -1)
+        pick = jnp.where(b <= 2 * low, near, b)
+        return jnp.where(z < planes - z, pick, planes - 1 - pick) if planes > 1 else z
+
+    order = [plane_at(b) for b in range(planes)]
+
+    def up_of(p):
+        return send(p * PLANE + q, p, 0, 0, me + PLANE)
+
+    def down_of(p):
+        return send(p * PLANE + q, p, 1, 0, me - PLANE)
+
+    def to_x(p):
+        return send(p * PLANE + q, p, 2, 1, z * PLANE + x_peer)
+
+    def to_y(p):
+        return send(p * PLANE + q, p, 3, 2, z * PLANE + y_peer)
+
+    def relay_y(p):
+        return send(p * PLANE + x_peer, p, 4, 3, z * PLANE + y_peer, 0, half)
+
+    def relay_x(p):
+        return send(p * PLANE + y_peer, p, 5, 4, z * PLANE + x_peer, half, half)
+
+    def wait_in(p, position, kind, first=0, count=None):
+        count = rows if count is None else count
+        part = gathered.at[p * PLANE + position, pl.ds(first, count)]
+        pltpu.make_async_copy(part, part, ag_recv.at[p, kind]).wait()
+
+    def column_stage(p):
+        @pl.when(p != z)
+        def _():
+            wait_in(p, q, 0)
+
+        @pl.when((p <= z) & (z < planes - 1))
+        def _():
+            up_of(p).start()
+
+        @pl.when((p >= z) & (z > 0))
+        def _():
+            down_of(p).start()
+
+        to_x(p).start()
+        to_y(p).start()
+
+    def relay_stage(p):
+        wait_in(p, x_peer, 1)
+        relay_y(p).start()
+        wait_in(p, y_peer, 2)
+        relay_x(p).start()
+
+    def diagonal_stage(p):
+        wait_in(p, d_peer, 3, 0, half)
+        wait_in(p, d_peer, 4, half, half)
+
+    def return_copy(group):
+        return pltpu.make_async_remote_copy(
+            src_ref=outgoing.at[group], dst_ref=incoming.at[me],
+            send_sem=ret_send.at[group], recv_sem=ret_recv.at[me],
+            device_id={"expert": group}, device_id_type=pl.DeviceIdType.MESH,
+        )
+
+    def own_return():
+        return pltpu.make_async_copy(outgoing.at[me], incoming.at[me], local_sem)
+
+    batch_tokens = PLANE * rows
+    batch_rows = PLANE * pad
+    t_i = lax.broadcasted_iota(jnp.int32, (batch_tokens, batch_tokens), 0)
+    t_j = lax.broadcasted_iota(jnp.int32, (batch_tokens, batch_tokens), 1)
+    before = ((t_j < t_i) & (t_j // rows == t_i // rows)).astype(jnp.bfloat16)
+    lane = lax.broadcasted_iota(jnp.int32, (batch_tokens, batch_rows), 1).astype(jnp.float32)
+    base = (
+        lax.broadcasted_iota(jnp.int32, (batch_tokens, batch_rows), 0) // rows * pad
+    ).astype(jnp.float32)
+    me_f = me.astype(jnp.float32)
+    ff_tile = tile_of(hidden, 256)
+    d_tile = tile_of(depth, 512)
+
+    def compute(p, first):
+        ids = gathered[pl.ds(p * PLANE, PLANE), :, depth:].reshape(batch_tokens, LANES)
+        hit = jnp.sum((ids.astype(jnp.float32) == me_f).astype(jnp.float32), axis=1, keepdims=True)
+        pos = jnp.dot(
+            before, jnp.broadcast_to(hit, (batch_tokens, batch_rows)).astype(jnp.bfloat16),
+            preferred_element_type=jnp.float32,
+        )
+        kept = (hit > 0.5) & (pos < cap - 0.5)
+        chosen = (kept & (lane == base + pos)).astype(jnp.float32)
+        load_ref[...] += jnp.sum(chosen)
+        chosen = chosen.astype(jnp.bfloat16)
+
+        @pl.loop(0, depth // d_tile)
+        def _(i):
+            cols = pl.ds(pl.multiple_of(i * d_tile, d_tile), d_tile)
+            block = gathered[pl.ds(p * PLANE, PLANE), :, cols].reshape(batch_tokens, d_tile)
+            packed[:, cols] = lax.dot_general(
+                chosen, block, (((0,), (0,)), ((), ())), preferred_element_type=jnp.float32
+            ).astype(jnp.bfloat16)
+
+        if first:
+            weight_copies[0].wait()
+            weight_copies[1].wait()
+
+        @pl.loop(0, hidden // ff_tile)
+        def _(i):
+            cols = pl.ds(pl.multiple_of(i * ff_tile, ff_tile), ff_tile)
+            gate = jnp.dot(packed[...], wg[:, cols], preferred_element_type=jnp.float32)
+            up = jnp.dot(packed[...], wu[:, cols], preferred_element_type=jnp.float32)
+            mid[:, cols] = (gate / (1.0 + jnp.exp(-gate)) * up).astype(jnp.bfloat16)
+
+        if first:
+            weight_copies[2].wait()
+
+        @pl.loop(0, depth // d_tile)
+        def _(i):
+            cols = pl.ds(pl.multiple_of(i * d_tile, d_tile), d_tile)
+            out = jnp.dot(mid[...], wd[:, cols], preferred_element_type=jnp.float32)
+            outgoing[pl.ds(p * PLANE, PLANE), :, :, cols] = out.reshape(
+                PLANE, outgoing.shape[1], outgoing.shape[2], d_tile
+            ).astype(jnp.bfloat16)
+
+        for j in range(PLANE):
+            group = p * PLANE + j
+
+            @pl.when(group != me)
+            def _():
+                return_copy(group).start()
+
+            @pl.when(group == me)
+            def _():
+                own_return().start()
+
+    load_ref[...] = jnp.zeros_like(load_ref)
+    column_stage(order[0])
+    relay_stage(order[0])
+    for b in range(planes):
+        if b + 1 < planes:
+            column_stage(order[b + 1])
+        diagonal_stage(order[b])
+        compute(order[b], b == 0)
+        if b + 1 < planes:
+            relay_stage(order[b + 1])
+    load_ref[...] = load_ref[...] * (n / (rows * n * top))
+
+    ids = gathered[me, :, depth:].astype(jnp.float32)
+    own_lane = lax.broadcasted_iota(jnp.int32, (rows, LANES), 1).astype(jnp.float32)
+    slots = [ids[:, k : k + 1] for k in range(top)]
+    hits = functools.reduce(jnp.add, [(s == own_lane).astype(jnp.float32) for s in slots])
+    r_i = lax.broadcasted_iota(jnp.int32, (rows, rows), 0)
+    r_j = lax.broadcasted_iota(jnp.int32, (rows, rows), 1)
+    positions = jnp.dot(
+        (r_j < r_i).astype(jnp.bfloat16), hits.astype(jnp.bfloat16),
+        preferred_element_type=jnp.float32,
+    )
+    columns, weights = [], []
+    for k in range(top):
+        at = jnp.sum(jnp.where(slots[k] == own_lane, positions, 0.0), axis=1, keepdims=True)
+        columns.append(slots[k] * pad + at)
+        weights.append(jnp.where(at < cap - 0.5, gates_ref[:, k : k + 1], 0.0))
+    col_lane = lax.broadcasted_iota(jnp.int32, (rows, batch_rows), 1).astype(jnp.float32)
+
+    for b in range(planes):
+        p = order[b]
+        for j in range(PLANE):
+            source = p * PLANE + j
+
+            @pl.when(source != me)
+            def _():
+                block = incoming.at[source]
+                pltpu.make_async_copy(block, block, ret_recv.at[source]).wait()
+
+            @pl.when(source == me)
+            def _():
+                own_return().wait()
+
+        shift = (p * batch_rows).astype(jnp.float32)
+        share = functools.reduce(
+            jnp.add,
+            [jnp.where(c - shift == col_lane, w, 0.0) for c, w in zip(columns, weights)],
+        )
+        high = share.astype(jnp.bfloat16)
+        rest = share - high.astype(jnp.float32)
+        middle = rest.astype(jnp.bfloat16)
+        low = (rest - middle.astype(jnp.float32)).astype(jnp.bfloat16)
+        spread = jnp.concatenate([high, middle, low], axis=0)
+
+        @pl.loop(0, depth // d_tile)
+        def _(i):
+            cols = pl.ds(pl.multiple_of(i * d_tile, d_tile), d_tile)
+            block = incoming[pl.ds(p * PLANE, PLANE), :, :, cols].astype(jnp.float32)
+            block = block.reshape(batch_rows, d_tile).astype(jnp.bfloat16)
+            sums = jnp.dot(spread, block, preferred_element_type=jnp.float32)
+            sums = sums[:rows] + (sums[rows : 2 * rows] + sums[2 * rows :])
+            if b > 0:
+                sums = acc[:, cols] + sums
+            if b < planes - 1:
+                acc[:, cols] = sums
+            else:
+                mixed_ref[:, cols] = sums.astype(jnp.bfloat16)
+
+    for b in range(planes):
+        p = order[b]
+
+        @pl.when((p <= z) & (z < planes - 1))
+        def _():
+            up_of(p).wait_send()
+
+        @pl.when((p >= z) & (z > 0))
+        def _():
+            down_of(p).wait_send()
+
+        to_x(p).wait_send()
+        to_y(p).wait_send()
+        relay_y(p).wait_send()
+        relay_x(p).wait_send()
+        for j in range(PLANE):
+            group = p * PLANE + j
+
+            @pl.when(group != me)
+            def _():
+                return_copy(group).wait_send()
+
+
+def per_device_gathered(
+    tokens, expert_ids, gate_weights, placement_table, replica_choice, w_gate, w_up, w_down
+):
+    n = lax.axis_size("expert")
+    rows, top = expert_ids.shape
+    depth = tokens.shape[1]
+    hidden = w_gate.shape[2]
+    cap = 5 * rows * top // (4 * n) + 1
+    slabs = -(-cap // 8)
+    experts = placement_table.shape[0]
+    pick = expert_ids[:, :, None] == jnp.arange(experts, dtype=jnp.int32)
+    both = jnp.where(
+        replica_choice[:, :, None] == 0, placement_table[:, 0], placement_table[:, 1]
+    )
+    slot_ids = jnp.sum(jnp.where(pick, both, 0), axis=2)
+    slot_cols = jnp.pad(
+        slot_ids.astype(tokens.dtype), ((0, 0), (0, LANES - top)), constant_values=-1
+    )
+    ext = jnp.concatenate([tokens, slot_cols], axis=1)
+    planes = n // PLANE
+    bf16, f32 = jnp.bfloat16, jnp.float32
+    anywhere = pl.BlockSpec(memory_space=pl.ANY)
+    vmem = pl.BlockSpec(memory_space=pltpu.VMEM)
+    mixed, load = pl.pallas_call(
+        functools.partial(kernel, n, rows, top, cap, depth, hidden),
+        out_shape=(
+            jax.ShapeDtypeStruct((rows, depth), bf16),
+            jax.ShapeDtypeStruct((8, LANES), f32),
+        ),
+        in_specs=[anywhere, vmem, anywhere, anywhere, anywhere],
+        out_specs=(vmem, vmem),
+        scratch_shapes=[
+            pltpu.VMEM((n, rows, depth + LANES), bf16),
+            pltpu.VMEM((depth, hidden), bf16),
+            pltpu.VMEM((depth, hidden), bf16),
+            pltpu.VMEM((hidden, depth), bf16),
+            pltpu.VMEM((PLANE * slabs * 8, depth), bf16),
+            pltpu.VMEM((PLANE * slabs * 8, hidden), bf16),
+            pltpu.VMEM((n, slabs, 8, depth), bf16),
+            pltpu.VMEM((n, slabs, 8, depth), bf16),
+            pltpu.VMEM((rows, depth), f32),
+            pltpu.SemaphoreType.DMA((3,)),
+            pltpu.SemaphoreType.DMA,
+            pltpu.SemaphoreType.DMA((planes, 6)),
+            pltpu.SemaphoreType.DMA((planes, 5)),
+            pltpu.SemaphoreType.DMA((n,)),
+            pltpu.SemaphoreType.DMA((n,)),
+            pltpu.SemaphoreType.DMA,
+        ],
+        compiler_params=pltpu.CompilerParams(
+            collective_id=0, has_side_effects=True, vmem_limit_bytes=VMEM_BYTES
+        ),
+    )(ext, gate_weights, w_gate, w_up, w_down)
+    return mixed, load[0, :1]
 
 
 def solution(mesh):
@@ -72,6 +409,17 @@
         P("expert", None, None),
         P("expert", None, None),
     )
+
+    def per_device(*args):
+        n = mesh.shape["expert"]
+        rows, depth = args[0].shape
+        weights = 3 * args[5].size
+        blocks = n * rows * (depth + LANES) + 2 * n * (rows + 8) * depth
+        fits = 2 * (weights + blocks) < 3 * VMEM_BYTES // 4
+        if fits and n % PLANE == 0 and n <= LANES and rows % 16 == 0:
+            return per_device_gathered(*args)
+        return per_device_exchange(*args)
+
     return jax.shard_map(
         per_device,
         mesh=mesh,

time: 213 us -> 129 us (0.61)
  blocking collectives: 151 us -> 0 us
  Pallas kernels: 0 us -> 118 us
  matrix products: 19.4 us -> 0 us
  local copies, waits for them, and re-layouts: 22.6 us -> 5.05 us
  starting transfers between devices: 8.67 us -> 0 us
  other arithmetic: 5.25 us -> 3.11 us
    pallas_call x0 -> x1, Pallas kernels: none -> 118 us  [per_device_gathered(): pl.pallas_call(functools.partial(kernel, n, rows, top, cap, depth, hidden...]
    unnamed x1 -> x0, blocking collectives: 82.5 us -> none
    all_to_all x1 -> x0, blocking collectives: 68.8 us -> none  [per_device(): lax.all_to_all(outgoing, 'expert', split_axis=0, concat_axis=0, tiled=True)]
    dot_general x2 -> x0, matrix products: 19.4 us -> none  [the longest x1 12.4 us: run_experts(): jnp.dot(hidden, down_w, preferred_element_type=jnp.float32)]
    reshape x4 -> x0, local copies, waits for them, and re-layouts: 9.63 us -> none  [the longest x1 3.23 us: run_experts(): return output.reshape(peers, capacity, hidden_dimension)]
    gather x3 -> x0, local copies, waits for them, and re-layouts: 9.16 us -> none  [the longest x1 3.77 us: per_device(): padded[source_item_index].reshape(devices, capacity, hidden_dimension)]
    all_to_all x1 -> x0, starting transfers between devices: 8.67 us -> none  [per_device(): lax.all_to_all(results, 'expert', split_axis=0, concat_axis=0, tiled=True)]
    reduce_sum x3 -> x1, other arithmetic: 3.85 us -> 0.78 us  [per_device_gathered(): slot_ids = jnp.sum(jnp.where(pick, both, 0), axis=2)]
  transfers between devices with their start and end apart: 1 -> 0, of which waited for: 0 -> 0; matrix products, arithmetic and copies ran while one was open for 1% -> 0% of each run, Pallas kernels for 0% -> 0%
where the time goes in v1:
time: 129 us; the launch traced here: 127 us
  Pallas kernels  118 us (91%)
  local copies, waits for them, and re-layouts  5.05 us (4%)
  other arithmetic  3.11 us (2%)
    pallas_call x1, Pallas kernels, per_device_gathered(): pl.pallas_call(functools.partial(kernel, n, rows, top, cap, depth, hidden...  118 us
    unnamed x2, local copies, waits for them, and re-layouts  3.01 us

profile of v1, /device:TPU:6, one launch (start us, length us, event | category | flops | bytes accessed | tf_op | source)
XLA Modules:
  0.0 127.0 jit_solution(11316967770598245348)
XLA Ops:
  0.6 0.7 broadcast_compare_fusion
  1.3 0.8 slice_bitcast_fusion.1
  2.1 0.8 select_reduce_fusion
  2.9 0.1 copy.15
  3.0 1.4 %copy.16.gates_ref = f32[32,8]{1,0:T(8,128)} copy(f32[32,8]{0,1:T(8,128)} %param.10) | data formatting | bytes 2048 | tf_op args[2]
  4.3 1.6 %fusion.1.ext_ref = bf16[32,3712]{1,0:T(8,128)(2,1)} fusion(bf16[32,8]{1,0:T(8,128)(2,1)S(1)} %copy.15, bf16[32,3584]{1,0:T(8,128)(2,1)} %param.8), kind=kLoop, calls=%fused_computation.2 | loop fusion | flops 712704 | bytes 467456 | tf_op jit(solution)/shard_map/concatenate | solution.py:363
  6.0 118.2 %shard_map.95 = (bf16[32,3584]{1,0:T(8,128)(2,1)}, f32[8,128]{1,0:T(8,128)}) custom-call(bf16[32,3712]{1,0:T(8,128)(2,1)} %fusion.1.ext_ref, f32[32,8]{1,0:T(8,128)} %copy.16.gates_ref, bf16[1,3584,1024]{2,1,0:T(8,128)(2,1)} %wg_hbm.1, bf16[1,3584,1024]{2,1,0:T(8,128)(2,1)} %wu_hbm.1, bf16[1,1024,3584]{2,1,0:T(8,128)(2,1)} %wd_hbm.1), custom_call_target="tpu_custom_call" | custom-call | tf_op jit(solution)/shard_map/pallas_call | solution.py:368
  124.2 1.2 slice.11
  125.4 1.6 %copy.18 = bf16[32,3584]{1,0:T(8,128)(2,1)} copy(bf16[32,3584]{1,0:T(8,128)(2,1)} %get-tuple-element.10) | data formatting | bytes 458752
  (1 shorter events, 0.0 us)

commit v2 on v1

--- a/solution.py
+++ b/solution.py
@@ -75,7 +75,7 @@
 
 def kernel(
     n, rows, top, cap, depth, hidden,
-    ext_ref, gates_ref, wg_hbm, wu_hbm, wd_hbm,
+    table_ref, tokens_hbm, ids_ref, choice_ref, gates_ref, wg_hbm, wu_hbm, wd_hbm,
     mixed_ref, load_ref,
     gathered, wg, wu, wd, packed, mid, outgoing, incoming, acc,
     w_sem, own_sem, ag_send, ag_recv, ret_send, ret_recv, local_sem,
@@ -95,8 +95,25 @@
         pltpu.make_async_copy(src.at[0], dst, w_sem.at[i])
         for i, (src, dst) in enumerate(((wg_hbm, wg), (wu_hbm, wu), (wd_hbm, wd)))
     ]
-    own = pltpu.make_async_copy(ext_ref, gathered.at[me], own_sem)
+    own = pltpu.make_async_copy(tokens_hbm, gathered.at[me, :, pl.ds(0, depth)], own_sem)
     own.start()
+    slot_rows = jnp.zeros((top, rows), jnp.int32)
+    for e in range(table_ref.shape[1]):
+        pair = jnp.where(choice_ref[...] == 0, table_ref[0, e], table_ref[1, e])
+        slot_rows = jnp.where(ids_ref[...] == e, pair, slot_rows)
+    eye = (
+        lax.broadcasted_iota(jnp.int32, (top, LANES), 0)
+        == lax.broadcasted_iota(jnp.int32, (top, LANES), 1)
+    ).astype(jnp.bfloat16)
+
+    def turned(block):
+        return lax.dot_general(
+            block, eye, (((0,), (0,)), ((), ())), preferred_element_type=jnp.float32
+        )
+
+    slot_cols = turned(slot_rows.astype(jnp.float32).astype(jnp.bfloat16))
+    k_lane = lax.broadcasted_iota(jnp.int32, (rows, LANES), 1)
+    gathered[me, :, depth:] = jnp.where(k_lane < top, slot_cols, -1.0).astype(jnp.bfloat16)
     for copy in weight_copies:
         copy.start()
 
@@ -118,13 +135,17 @@
             device_id={"expert": target}, device_id_type=pl.DeviceIdType.MESH,
         )
 
+    z_half = planes // 2
+    low = jnp.minimum(z, planes - 1 - z)
+
     def plane_at(b):
-        low = jnp.minimum(z, planes - 1 - z)
-        near = low + ((b + 1) // 2) * (1 if b % 2 else -1)
-        pick = jnp.where(b <= 2 * low, near, b)
-        return jnp.where(z < planes - z, pick, planes - 1 - pick) if planes > 1 else z
+        pick = lax.rem(low + b, planes)
+        return jnp.where(z < z_half, pick, planes - 1 - pick)
 
     order = [plane_at(b) for b in range(planes)]
+
+    def across(p):
+        return (p // z_half) != (z // z_half)
 
     def up_of(p):
         return send(p * PLANE + q, p, 0, 0, me + PLANE)
@@ -149,19 +170,24 @@
         part = gathered.at[p * PLANE + position, pl.ds(first, count)]
         pltpu.make_async_copy(part, part, ag_recv.at[p, kind]).wait()
 
-    def column_stage(p):
-        @pl.when(p != z)
+    def column_stage(d):
+        @pl.when(z - d >= 0)
         def _():
-            wait_in(p, q, 0)
-
-        @pl.when((p <= z) & (z < planes - 1))
+            wait_in(z - d, q, 0)
+
+            @pl.when(z < planes - 1)
+            def _():
+                up_of(z - d).start()
+
+        @pl.when(z + d < planes)
         def _():
-            up_of(p).start()
-
-        @pl.when((p >= z) & (z > 0))
-        def _():
-            down_of(p).start()
-
+            wait_in(z + d, q, 0)
+
+            @pl.when(z > 0)
+            def _():
+                down_of(z + d).start()
+
+    def spread_stage(p):
         to_x(p).start()
         to_y(p).start()
 
@@ -207,7 +233,7 @@
         )
         kept = (hit > 0.5) & (pos < cap - 0.5)
         chosen = (kept & (lane == base + pos)).astype(jnp.float32)
-        load_ref[...] += jnp.sum(chosen)
+        chosen_count = chosen
         chosen = chosen.astype(jnp.bfloat16)
 
         @pl.loop(0, depth // d_tile)
@@ -240,6 +266,9 @@
                 PLANE, outgoing.shape[1], outgoing.shape[2], d_tile
             ).astype(jnp.bfloat16)
 
+        return jnp.sum(chosen_count)
+
+    def give_back(p):
         for j in range(PLANE):
             group = p * PLANE + j
 
@@ -251,21 +280,54 @@
             def _():
                 own_return().start()
 
-    load_ref[...] = jnp.zeros_like(load_ref)
-    column_stage(order[0])
+    accepted = jnp.float32(0.0)
+
+    @pl.when(z < planes - 1)
+    def _():
+        up_of(z).start()
+
+    @pl.when(z > 0)
+    def _():
+        down_of(z).start()
+
+    spread_stage(order[0])
+    column_stage(1)
+    spread_stage(order[1])
     relay_stage(order[0])
+    for d in range(2, planes - 1):
+        column_stage(d)
     for b in range(planes):
-        if b + 1 < planes:
-            column_stage(order[b + 1])
+        if b == 1:
+            column_stage(planes - 1)
+        if 0 < b < planes - 1:
+            spread_stage(order[b + 1])
         diagonal_stage(order[b])
-        compute(order[b], b == 0)
-        if b + 1 < planes:
+        accepted += compute(order[b], b == 0)
+        if b < planes - 1:
+
+            @pl.when(across(order[b]))
+            def _():
+                give_back(order[b])
+
             relay_stage(order[b + 1])
-    load_ref[...] = load_ref[...] * (n / (rows * n * top))
-
-    ids = gathered[me, :, depth:].astype(jnp.float32)
+        else:
+            give_back(order[b])
+        if b == planes - 2:
+            for c in range(planes - 1):
+
+                @pl.when(jnp.logical_not(across(order[c])))
+                def _():
+                    give_back(order[c])
+
+    load_ref[0] = accepted * (n / (rows * n * top))
+
+    g_high = gates_ref[...].astype(jnp.bfloat16)
+    g_rest = gates_ref[...] - g_high.astype(jnp.float32)
+    g_middle = g_rest.astype(jnp.bfloat16)
+    g_low = (g_rest - g_middle.astype(jnp.float32)).astype(jnp.bfloat16)
+    gate_cols = turned(g_high) + (turned(g_middle) + turned(g_low))
     own_lane = lax.broadcasted_iota(jnp.int32, (rows, LANES), 1).astype(jnp.float32)
-    slots = [ids[:, k : k + 1] for k in range(top)]
+    slots = [slot_cols[:, k : k + 1] for k in range(top)]
     hits = functools.reduce(jnp.add, [(s == own_lane).astype(jnp.float32) for s in slots])
     r_i = lax.broadcasted_iota(jnp.int32, (rows, rows), 0)
     r_j = lax.broadcasted_iota(jnp.int32, (rows, rows), 1)
@@ -277,11 +339,14 @@
     for k in range(top):
         at = jnp.sum(jnp.where(slots[k] == own_lane, positions, 0.0), axis=1, keepdims=True)
         columns.append(slots[k] * pad + at)
-        weights.append(jnp.where(at < cap - 0.5, gates_ref[:, k : k + 1], 0.0))
+        weights.append(jnp.where(at < cap - 0.5, gate_cols[:, k : k + 1], 0.0))
     col_lane = lax.broadcasted_iota(jnp.int32, (rows, batch_rows), 1).astype(jnp.float32)
 
-    for b in range(planes):
-        p = order[b]
+    for step in range(planes):
+        turn = lax.rem(z // z_half + 1 + step // z_half, 2)
+        turn = 1 - turn
+        inner = step % z_half
+        p = turn * z_half + jnp.where(turn == 0, z_half - 1 - inner, inner)
         for j in range(PLANE):
             source = p * PLANE + j
 
@@ -312,9 +377,9 @@
             block = block.reshape(batch_rows, d_tile).astype(jnp.bfloat16)
             sums = jnp.dot(spread, block, preferred_element_type=jnp.float32)
             sums = sums[:rows] + (sums[rows : 2 * rows] + sums[2 * rows :])
-            if b > 0:
+            if step > 0:
                 sums = acc[:, cols] + sums
-            if b < planes - 1:
+            if step < planes - 1:
                 acc[:, cols] = sums
             else:
                 mixed_ref[:, cols] = sums.astype(jnp.bfloat16)
@@ -351,28 +416,19 @@
     hidden = w_gate.shape[2]
     cap = 5 * rows * top // (4 * n) + 1
     slabs = -(-cap // 8)
-    experts = placement_table.shape[0]
-    pick = expert_ids[:, :, None] == jnp.arange(experts, dtype=jnp.int32)
-    both = jnp.where(
-        replica_choice[:, :, None] == 0, placement_table[:, 0], placement_table[:, 1]
-    )
-    slot_ids = jnp.sum(jnp.where(pick, both, 0), axis=2)
-    slot_cols = jnp.pad(
-        slot_ids.astype(tokens.dtype), ((0, 0), (0, LANES - top)), constant_values=-1
-    )
-    ext = jnp.concatenate([tokens, slot_cols], axis=1)
     planes = n // PLANE
     bf16, f32 = jnp.bfloat16, jnp.float32
     anywhere = pl.BlockSpec(memory_space=pl.ANY)
     vmem = pl.BlockSpec(memory_space=pltpu.VMEM)
+    smem = pl.BlockSpec(memory_space=pltpu.SMEM)
     mixed, load = pl.pallas_call(
         functools.partial(kernel, n, rows, top, cap, depth, hidden),
         out_shape=(
             jax.ShapeDtypeStruct((rows, depth), bf16),
-            jax.ShapeDtypeStruct((8, LANES), f32),
+            jax.ShapeDtypeStruct((1,), f32),
         ),
-        in_specs=[anywhere, vmem, anywhere, anywhere, anywhere],
-        out_specs=(vmem, vmem),
+        in_specs=[smem, anywhere, vmem, vmem, vmem, anywhere, anywhere, anywhere],
+        out_specs=(vmem, smem),
         scratch_shapes=[
             pltpu.VMEM((n, rows, depth + LANES), bf16),
             pltpu.VMEM((depth, hidden), bf16),
@@ -394,8 +450,11 @@
         compiler_params=pltpu.CompilerParams(
             collective_id=0, has_side_effects=True, vmem_limit_bytes=VMEM_BYTES
         ),
-    )(ext, gate_weights, w_gate, w_up, w_down)
-    return mixed, load[0, :1]
+    )(
+        placement_table.T, tokens, expert_ids.T, replica_choice.T, gate_weights.T,
+        w_gate, w_up, w_down,
+    )
+    return mixed, load
 
 
 def solution(mesh):
@@ -416,7 +475,7 @@
         weights = 3 * args[5].size
         blocks = n * rows * (depth + LANES) + 2 * n * (rows + 8) * depth
         fits = 2 * (weights + blocks) < 3 * VMEM_BYTES // 4
-        if fits and n % PLANE == 0 and n <= LANES and rows % 16 == 0:
+        if fits and n % (2 * PLANE) == 0 and n <= LANES and rows % 16 == 0:
             return per_device_gathered(*args)
         return per_device_exchange(*args)
 

time: 129 us -> 123 us (0.953); the launches traced: 127 us -> 122 us
  local copies, waits for them, and re-layouts: 5.05 us -> 1.64 us
  other arithmetic: 3.11 us -> 0 us
  between operations: 0.65 us -> 2.4 us
    concatenate x1 -> x0, other arithmetic: 1.63 us -> none  [per_device_gathered(): ext = jnp.concatenate([tokens, slot_cols], axis=1)]
    unnamed x2 -> x1, local copies, waits for them, and re-layouts: 3.01 us -> 1.64 us
where the time goes in v2:
time: 123 us; the launch traced here: 122 us
  Pallas kernels  118 us (96%)
  between operations  2.4 us (2%)
  local copies, waits for them, and re-layouts  1.64 us (1%)
    pallas_call x1, Pallas kernels, per_device_gathered(): pl.pallas_call(functools.partial(kernel, n, rows, top, cap, depth, hidden...  118 us

profile of v2, /device:TPU:6, one launch (start us, length us, event | category | flops | bytes accessed | tf_op | source)
XLA Modules:
  0.0 122.3 jit_solution(15559428955306515739)
XLA Ops:
  0.6 118.3 %shard_map.95 = (bf16[32,3584]{1,0:T(8,128)(2,1)}, f32[1]{0:T(128)}) custom-call(s32[2,12]{1,0:T(2,128)} %bitcast.7, bf16[32,3584]{1,0:T(8,128)(2,1)} %tokens_hbm.1, s32[8,32]{1,0:T(8,128)} %bitcast.4, s32[8,32]{1,0:T(8,128)} %bitcast.5, f32[8,32]{1,0:T(8,128)} %bitcast.6, bf16[1,3584,1024]{2,1,0:T(8,128)(2,1)} %wg_hbm.1, bf16[1,3584,1024]{2,1,0:T(8,128)(2,1)} %wu_hbm.1, ...), custom_call_target="tpu_custom_call" | custom-call | tf_op jit(solution)/shard_map/pallas_call | solution.py:424
  118.9 1.6 %copy.12 = bf16[32,3584]{1,0:T(8,128)(2,1)} copy(bf16[32,3584]{1,0:T(8,128)(2,1)} %get-tuple-element.4) | data formatting | bytes 458752

commit v3 on v2

--- a/solution.py
+++ b/solution.py
@@ -294,30 +294,30 @@
     column_stage(1)
     spread_stage(order[1])
     relay_stage(order[0])
-    for d in range(2, planes - 1):
-        column_stage(d)
-    for b in range(planes):
-        if b == 1:
-            column_stage(planes - 1)
-        if 0 < b < planes - 1:
-            spread_stage(order[b + 1])
+    column_stage(2)
+    relay_stage(order[1])
+    spread_stage(order[2])
+    turns = [1, 0] + list(range(2, planes))
+    for i, b in enumerate(turns):
         diagonal_stage(order[b])
-        accepted += compute(order[b], b == 0)
-        if b < planes - 1:
-
-            @pl.when(across(order[b]))
-            def _():
-                give_back(order[b])
-
-            relay_stage(order[b + 1])
-        else:
+        accepted += compute(order[b], i == 0)
+
+        @pl.when(across(order[b]))
+        def _():
             give_back(order[b])
-        if b == planes - 2:
-            for c in range(planes - 1):
-
-                @pl.when(jnp.logical_not(across(order[c])))
-                def _():
-                    give_back(order[c])
+
+        if i + 3 < planes:
+            column_stage(i + 3)
+            relay_stage(order[i + 2])
+            spread_stage(order[i + 3])
+        elif i + 2 < planes:
+            relay_stage(order[i + 2])
+
+    for b in turns:
+
+        @pl.when(jnp.logical_not(across(order[b])))
+        def _():
+            give_back(order[b])
 
     load_ref[0] = accepted * (n / (rows * n * top))
 
@@ -475,7 +475,7 @@
         weights = 3 * args[5].size
         blocks = n * rows * (depth + LANES) + 2 * n * (rows + 8) * depth
         fits = 2 * (weights + blocks) < 3 * VMEM_BYTES // 4
-        if fits and n % (2 * PLANE) == 0 and n <= LANES and rows % 16 == 0:
+        if fits and n % (2 * PLANE) == 0 and n > 2 * PLANE and n <= LANES and rows % 16 == 0:
             return per_device_gathered(*args)
         return per_device_exchange(*args)
 

time: 123 us -> 115 us (0.935)
  Pallas kernels: 118 us -> 111 us
    pallas_call x1, Pallas kernels: 118 us -> 111 us  [per_device_gathered(): pl.pallas_call(functools.partial(kernel, n, rows, top, cap, depth, hidden...]
where the time goes in v3:
time: 115 us
  Pallas kernels  111 us (97%)
  between operations  2.4 us (2%)
  local copies, waits for them, and re-layouts  1.64 us (1%)
    pallas_call x1, Pallas kernels, per_device_gathered(): pl.pallas_call(functools.partial(kernel, n, rows, top, cap, depth, hidden...  111 us

profile of v3, /device:TPU:6, one launch (start us, length us, event | category | flops | bytes accessed | tf_op | source)
XLA Modules:
  0.0 114.8 jit_solution(7940421536871079114)
XLA Ops:
  0.6 110.8 %shard_map.95 = (bf16[32,3584]{1,0:T(8,128)(2,1)}, f32[1]{0:T(128)}) custom-call(s32[2,12]{1,0:T(2,128)} %bitcast.7, bf16[32,3584]{1,0:T(8,128)(2,1)} %tokens_hbm.1, s32[8,32]{1,0:T(8,128)} %bitcast.4, s32[8,32]{1,0:T(8,128)} %bitcast.5, f32[8,32]{1,0:T(8,128)} %bitcast.6, bf16[1,3584,1024]{2,1,0:T(8,128)(2,1)} %wg_hbm.1, bf16[1,3584,1024]{2,1,0:T(8,128)(2,1)} %wu_hbm.1, ...), custom_call_target="tpu_custom_call" | custom-call | tf_op jit(solution)/shard_map/pallas_call | solution.py:424
  111.4 1.6 %copy.12 = bf16[32,3584]{1,0:T(8,128)(2,1)} copy(bf16[32,3584]{1,0:T(8,128)(2,1)} %get-tuple-element.4) | data formatting | bytes 458752

commit v4 on v3

--- a/solution.py
+++ b/solution.py
@@ -9,6 +9,7 @@
 
 PLANE = 4
 LANES = 128
+D_TILE = 256
 VMEM_BYTES = 64 * 1000 * 1000
 
 
@@ -73,15 +74,29 @@
     return tile
 
 
+def folds_of(cap, depth, tile):
+    full = cap // 8
+    offset, first, pieces = full * depth, full * 8, []
+    for count in (4, 2, 1):
+        if cap % 8 & count:
+            folds = max(f for f in range(1, 8 // count + 1) if depth // tile % f == 0)
+            width = depth // folds
+            pieces.append((first, count, folds, width, offset))
+            first, offset = first + count, offset + width
+    return full, pieces, offset
+
+
 def kernel(
     n, rows, top, cap, depth, hidden,
     table_ref, tokens_hbm, ids_ref, choice_ref, gates_ref, wg_hbm, wu_hbm, wd_hbm,
     mixed_ref, load_ref,
-    gathered, wg, wu, wd, packed, mid, outgoing, incoming, acc,
+    gathered, wg, wu, wd, packed, mid, outgoing, incoming, acc, folded,
     w_sem, own_sem, ag_send, ag_recv, ret_send, ret_recv, local_sem,
 ):
     planes = n // PLANE
-    pad = outgoing.shape[1] * outgoing.shape[2]
+    pad = packed.shape[0] // PLANE
+    d_tile = tile_of(depth, D_TILE)
+    full, pieces, _ = folds_of(cap, depth, d_tile)
     me = lax.axis_index("expert")
     z = me // PLANE
     q = me % PLANE
@@ -101,6 +116,7 @@
     for e in range(table_ref.shape[1]):
         pair = jnp.where(choice_ref[...] == 0, table_ref[0, e], table_ref[1, e])
         slot_rows = jnp.where(ids_ref[...] == e, pair, slot_rows)
+    folded[...] = jnp.zeros_like(folded)
     eye = (
         lax.broadcasted_iota(jnp.int32, (top, LANES), 0)
         == lax.broadcasted_iota(jnp.int32, (top, LANES), 1)
@@ -222,7 +238,6 @@
     ).astype(jnp.float32)
     me_f = me.astype(jnp.float32)
     ff_tile = tile_of(hidden, 256)
-    d_tile = tile_of(depth, 512)
 
     def compute(p, first):
         ids = gathered[pl.ds(p * PLANE, PLANE), :, depth:].reshape(batch_tokens, LANES)
@@ -262,10 +277,26 @@
         def _(i):
             cols = pl.ds(pl.multiple_of(i * d_tile, d_tile), d_tile)
             out = jnp.dot(mid[...], wd[:, cols], preferred_element_type=jnp.float32)
-            outgoing[pl.ds(p * PLANE, PLANE), :, :, cols] = out.reshape(
-                PLANE, outgoing.shape[1], outgoing.shape[2], d_tile
-            ).astype(jnp.bfloat16)
-
+            out = out.reshape(PLANE, pad, d_tile)
+            for slab in range(full):
+                at = pl.ds(pl.multiple_of(slab * depth + i * d_tile, d_tile), d_tile)
+                outgoing[pl.ds(p * PLANE, PLANE), :, at] = out[
+                    :, slab * 8 : slab * 8 + 8
+                ].astype(jnp.bfloat16)
+            for start, count, _, width, offset in pieces:
+                steps = width // d_tile
+                at = pl.ds(
+                    pl.multiple_of(offset - full * depth + i % steps * d_tile, d_tile), d_tile
+                )
+                for r in range(count):
+                    folded[:, pl.ds(i // steps * count + r, 1), at] = out[
+                        :, start + r : start + r + 1
+                    ]
+
+        if pieces:
+            outgoing[pl.ds(p * PLANE, PLANE), :, full * depth :] = folded[...].astype(
+                jnp.bfloat16
+            )
         return jnp.sum(chosen_count)
 
     def give_back(p):
@@ -335,12 +366,20 @@
         (r_j < r_i).astype(jnp.bfloat16), hits.astype(jnp.bfloat16),
         preferred_element_type=jnp.float32,
     )
-    columns, weights = [], []
+    columns, weights, inside_plane = [], [], []
     for k in range(top):
         at = jnp.sum(jnp.where(slots[k] == own_lane, positions, 0.0), axis=1, keepdims=True)
-        columns.append(slots[k] * pad + at)
+        lane_of = at + (PLANE * 8 - 8) * jnp.floor(at * 0.125)
+        moves = []
+        for index, (start, count, _, _, _) in enumerate(pieces):
+            inside = (at > start - 0.5) & (at < start + count - 0.5)
+            lane_of = jnp.where(inside, (full + index) * PLANE * 8 + at - start, lane_of)
+            moves.append(jnp.where(inside, float(count), 0.0))
+        columns.append((slots[k] * 8 + lane_of, moves))
         weights.append(jnp.where(at < cap - 0.5, gate_cols[:, k : k + 1], 0.0))
-    col_lane = lax.broadcasted_iota(jnp.int32, (rows, batch_rows), 1).astype(jnp.float32)
+        inside_plane.append(jnp.floor(slots[k] * (1.0 / PLANE)))
+    stacked = (full + len(pieces)) * PLANE * 8
+    col_lane = lax.broadcasted_iota(jnp.int32, (rows, stacked), 1).astype(jnp.float32)
 
     for step in range(planes):
         turn = lax.rem(z // z_half + 1 + step // z_half, 2)
@@ -359,22 +398,36 @@
             def _():
                 own_return().wait()
 
-        shift = (p * batch_rows).astype(jnp.float32)
-        share = functools.reduce(
-            jnp.add,
-            [jnp.where(c - shift == col_lane, w, 0.0) for c, w in zip(columns, weights)],
-        )
-        high = share.astype(jnp.bfloat16)
-        rest = share - high.astype(jnp.float32)
-        middle = rest.astype(jnp.bfloat16)
-        low = (rest - middle.astype(jnp.float32)).astype(jnp.bfloat16)
-        spread = jnp.concatenate([high, middle, low], axis=0)
+        p_f = p.astype(jnp.float32)
+        here = [jnp.where(g == p_f, w, 0.0) for g, w in zip(inside_plane, weights)]
 
         @pl.loop(0, depth // d_tile)
         def _(i):
             cols = pl.ds(pl.multiple_of(i * d_tile, d_tile), d_tile)
-            block = incoming[pl.ds(p * PLANE, PLANE), :, :, cols].astype(jnp.float32)
-            block = block.reshape(batch_rows, d_tile).astype(jnp.bfloat16)
+            offsets = [slab * depth + i * d_tile for slab in range(full)]
+            shifts = []
+            for _, _, _, width, offset in pieces:
+                steps = width // d_tile
+                offsets.append(offset + i % steps * d_tile)
+                shifts.append((i // steps).astype(jnp.float32))
+            share = jnp.zeros((rows, stacked), jnp.float32)
+            for (lane_of, moves), w in zip(columns, here):
+                at = lane_of - p_f * (PLANE * 8)
+                for move, shift in zip(moves, shifts):
+                    at = at + move * shift
+                share = share + jnp.where(at == col_lane, w, 0.0)
+            high = share.astype(jnp.bfloat16)
+            rest = share - high.astype(jnp.float32)
+            middle = rest.astype(jnp.bfloat16)
+            low = (rest - middle.astype(jnp.float32)).astype(jnp.bfloat16)
+            spread = jnp.concatenate([high, middle, low], axis=0)
+            slabs = [
+                incoming[
+                    pl.ds(p * PLANE, PLANE), :, pl.ds(pl.multiple_of(o, d_tile), d_tile)
+                ].astype(jnp.float32).reshape(PLANE * 8, d_tile)
+                for o in offsets
+            ]
+            block = jnp.concatenate(slabs, axis=0).astype(jnp.bfloat16)
             sums = jnp.dot(spread, block, preferred_element_type=jnp.float32)
             sums = sums[:rows] + (sums[rows : 2 * rows] + sums[2 * rows :])
             if step > 0:
@@ -416,6 +469,7 @@
     hidden = w_gate.shape[2]
     cap = 5 * rows * top // (4 * n) + 1
     slabs = -(-cap // 8)
+    _, _, length = folds_of(cap, depth, tile_of(depth, D_TILE))
     planes = n // PLANE
     bf16, f32 = jnp.bfloat16, jnp.float32
     anywhere = pl.BlockSpec(memory_space=pl.ANY)
@@ -436,9 +490,10 @@
             pltpu.VMEM((hidden, depth), bf16),
             pltpu.VMEM((PLANE * slabs * 8, depth), bf16),
             pltpu.VMEM((PLANE * slabs * 8, hidden), bf16),
-            pltpu.VMEM((n, slabs, 8, depth), bf16),
-            pltpu.VMEM((n, slabs, 8, depth), bf16),
+            pltpu.VMEM((n, 8, length), bf16),
+            pltpu.VMEM((n, 8, length), bf16),
             pltpu.VMEM((rows, depth), f32),
+            pltpu.VMEM((PLANE, 8, max(length - cap // 8 * depth, LANES)), f32),
             pltpu.SemaphoreType.DMA((3,)),
             pltpu.SemaphoreType.DMA,
             pltpu.SemaphoreType.DMA((planes, 6)),

time: 115 us -> 127 us (1.10)
  Pallas kernels: 111 us -> 123 us
    pallas_call x1, Pallas kernels: 111 us -> 123 us  [per_device_gathered(): pl.pallas_call(functools.partial(kernel, n, rows, top, cap, depth, hidden...]
where the time goes in v4:
time: 127 us
  Pallas kernels  123 us (97%)
  between operations  2.4 us (2%)
  local copies, waits for them, and re-layouts  1.64 us (1%)
    pallas_call x1, Pallas kernels, per_device_gathered(): pl.pallas_call(functools.partial(kernel, n, rows, top, cap, depth, hidden...  123 us

profile of v4, /device:TPU:6, one launch (start us, length us, event | category | flops | bytes accessed | tf_op | source)
XLA Modules:
  0.0 127.0 jit_solution(13788873707156522450)
XLA Ops:
  0.6 123.0 %shard_map.95 = (bf16[32,3584]{1,0:T(8,128)(2,1)}, f32[1]{0:T(128)}) custom-call(s32[2,12]{1,0:T(2,128)} %bitcast.7, bf16[32,3584]{1,0:T(8,128)(2,1)} %tokens_hbm.1, s32[8,32]{1,0:T(8,128)} %bitcast.4, s32[8,32]{1,0:T(8,128)} %bitcast.5, f32[8,32]{1,0:T(8,128)} %bitcast.6, bf16[1,3584,1024]{2,1,0:T(8,128)(2,1)} %wg_hbm.1, bf16[1,3584,1024]{2,1,0:T(8,128)(2,1)} %wu_hbm.1, ...), custom_call_target="tpu_custom_call" | custom-call | tf_op jit(solution)/shard_map/pallas_call | solution.py:478
  123.6 1.6 %copy.12 = bf16[32,3584]{1,0:T(8,128)(2,1)} copy(bf16[32,3584]{1,0:T(8,128)(2,1)} %get-tuple-element.4) | data formatting | bytes 458752

commit v5 on v4

--- a/solution.py
+++ b/solution.py
@@ -90,7 +90,7 @@
     n, rows, top, cap, depth, hidden,
     table_ref, tokens_hbm, ids_ref, choice_ref, gates_ref, wg_hbm, wu_hbm, wd_hbm,
     mixed_ref, load_ref,
-    gathered, wg, wu, wd, packed, mid, outgoing, incoming, acc, folded,
+    gathered, wg, wu, wd, packed, mid, outgoing, incoming, acc, folded, spreads,
     w_sem, own_sem, ag_send, ag_recv, ret_send, ret_recv, local_sem,
 ):
     planes = n // PLANE
@@ -251,7 +251,7 @@
         chosen_count = chosen
         chosen = chosen.astype(jnp.bfloat16)
 
-        @pl.loop(0, depth // d_tile)
+        @pl.loop(0, depth // d_tile, unroll=2)
         def _(i):
             cols = pl.ds(pl.multiple_of(i * d_tile, d_tile), d_tile)
             block = gathered[pl.ds(p * PLANE, PLANE), :, cols].reshape(batch_tokens, d_tile)
@@ -273,7 +273,7 @@
         if first:
             weight_copies[2].wait()
 
-        @pl.loop(0, depth // d_tile)
+        @pl.loop(0, depth // d_tile, unroll=2)
         def _(i):
             cols = pl.ds(pl.multiple_of(i * d_tile, d_tile), d_tile)
             out = jnp.dot(mid[...], wd[:, cols], preferred_element_type=jnp.float32)
@@ -381,35 +381,16 @@
     stacked = (full + len(pieces)) * PLANE * 8
     col_lane = lax.broadcasted_iota(jnp.int32, (rows, stacked), 1).astype(jnp.float32)
 
-    for step in range(planes):
-        turn = lax.rem(z // z_half + 1 + step // z_half, 2)
-        turn = 1 - turn
-        inner = step % z_half
-        p = turn * z_half + jnp.where(turn == 0, z_half - 1 - inner, inner)
-        for j in range(PLANE):
-            source = p * PLANE + j
-
-            @pl.when(source != me)
-            def _():
-                block = incoming.at[source]
-                pltpu.make_async_copy(block, block, ret_recv.at[source]).wait()
-
-            @pl.when(source == me)
-            def _():
-                own_return().wait()
-
+    @pl.loop(0, planes)
+    def _(p):
         p_f = p.astype(jnp.float32)
         here = [jnp.where(g == p_f, w, 0.0) for g, w in zip(inside_plane, weights)]
 
         @pl.loop(0, depth // d_tile)
         def _(i):
-            cols = pl.ds(pl.multiple_of(i * d_tile, d_tile), d_tile)
-            offsets = [slab * depth + i * d_tile for slab in range(full)]
-            shifts = []
-            for _, _, _, width, offset in pieces:
-                steps = width // d_tile
-                offsets.append(offset + i % steps * d_tile)
-                shifts.append((i // steps).astype(jnp.float32))
+            shifts = [
+                (i // (width // d_tile)).astype(jnp.float32) for _, _, _, width, _ in pieces
+            ]
             share = jnp.zeros((rows, stacked), jnp.float32)
             for (lane_of, moves), w in zip(columns, here):
                 at = lane_of - p_f * (PLANE * 8)
@@ -420,7 +401,33 @@
             rest = share - high.astype(jnp.float32)
             middle = rest.astype(jnp.bfloat16)
             low = (rest - middle.astype(jnp.float32)).astype(jnp.bfloat16)
-            spread = jnp.concatenate([high, middle, low], axis=0)
+            spreads[p, i] = jnp.concatenate([high, middle, low], axis=0)
+
+    for step in range(planes):
+        turn = lax.rem(z // z_half + 1 + step // z_half, 2)
+        turn = 1 - turn
+        inner = step % z_half
+        p = turn * z_half + jnp.where(turn == 0, z_half - 1 - inner, inner)
+        for j in range(PLANE):
+            source = p * PLANE + j
+
+            @pl.when(source != me)
+            def _():
+                block = incoming.at[source]
+                pltpu.make_async_copy(block, block, ret_recv.at[source]).wait()
+
+            @pl.when(source == me)
+            def _():
+                own_return().wait()
+
+
+        @pl.loop(0, depth // d_tile, unroll=2)
+        def _(i):
+            cols = pl.ds(pl.multiple_of(i * d_tile, d_tile), d_tile)
+            offsets = [slab * depth + i * d_tile for slab in range(full)]
+            for _, _, _, width, offset in pieces:
+                offsets.append(offset + i % (width // d_tile) * d_tile)
+            spread = spreads[p, i]
             slabs = [
                 incoming[
                     pl.ds(p * PLANE, PLANE), :, pl.ds(pl.multiple_of(o, d_tile), d_tile)
@@ -469,7 +476,9 @@
     hidden = w_gate.shape[2]
     cap = 5 * rows * top // (4 * n) + 1
     slabs = -(-cap // 8)
-    _, _, length = folds_of(cap, depth, tile_of(depth, D_TILE))
+    d_tile = tile_of(depth, D_TILE)
+    full, pieces, length = folds_of(cap, depth, d_tile)
+    stacked = (full + len(pieces)) * PLANE * 8
     planes = n // PLANE
     bf16, f32 = jnp.bfloat16, jnp.float32
     anywhere = pl.BlockSpec(memory_space=pl.ANY)
@@ -494,6 +503,7 @@
             pltpu.VMEM((n, 8, length), bf16),
             pltpu.VMEM((rows, depth), f32),
             pltpu.VMEM((PLANE, 8, max(length - cap // 8 * depth, LANES)), f32),
+            pltpu.VMEM((planes, depth // d_tile, 3 * rows, stacked), bf16),
             pltpu.SemaphoreType.DMA((3,)),
             pltpu.SemaphoreType.DMA,
             pltpu.SemaphoreType.DMA((planes, 6)),

time: 127 us -> 108 us (0.85)
  Pallas kernels: 123 us -> 104 us
    pallas_call x1, Pallas kernels: 123 us -> 104 us  [per_device_gathered(): pl.pallas_call(functools.partial(kernel, n, rows, top, cap, depth, hidden...]
where the time goes in v5:
time: 108 us
  Pallas kernels  104 us (96%)
  between operations  2.4 us (2%)
  local copies, waits for them, and re-layouts  1.64 us (2%)
    pallas_call x1, Pallas kernels, per_device_gathered(): pl.pallas_call(functools.partial(kernel, n, rows, top, cap, depth, hidden...  104 us

profile of v5, /device:TPU:6, one launch (start us, length us, event | category | flops | bytes accessed | tf_op | source)
XLA Modules:
  0.0 107.6 jit_solution(9928531206529545757)
XLA Ops:
  0.6 103.6 %shard_map.95 = (bf16[32,3584]{1,0:T(8,128)(2,1)}, f32[1]{0:T(128)}) custom-call(s32[2,12]{1,0:T(2,128)} %bitcast.7, bf16[32,3584]{1,0:T(8,128)(2,1)} %tokens_hbm.1, s32[8,32]{1,0:T(8,128)} %bitcast.4, s32[8,32]{1,0:T(8,128)} %bitcast.5, f32[8,32]{1,0:T(8,128)} %bitcast.6, bf16[1,3584,1024]{2,1,0:T(8,128)(2,1)} %wg_hbm.1, bf16[1,3584,1024]{2,1,0:T(8,128)(2,1)} %wu_hbm.1, ...), custom_call_target="tpu_custom_call" | custom-call | tf_op jit(solution)/shard_map/pallas_call | solution.py:487
  104.2 1.6 %copy.12 = bf16[32,3584]{1,0:T(8,128)(2,1)} copy(bf16[32,3584]{1,0:T(8,128)(2,1)} %get-tuple-element.4) | data formatting | bytes 458752
